TPU v7x, 32 devices: a whole 2x2x4 slice. The times are simulated.
32 devices in a mesh: pod: 2 (over x), dp: 4 (over z), sp: 4 (over y, core).
Axes of the slice: x: 2, y: 2, z: 4, core: 2. Of those that a mesh axis runs over, the one named last changes fastest.
Arguments:
- images: bfloat16 [24, 512, 64, 64], P(('pod', 'dp'), 'sp'), parts along dimension 0
- w_a: bfloat16 [1, 3, 3, 64, 64], replicated
- norm_a: float32 [1, 2, 64], replicated
- w_down: bfloat16 [3, 3, 64, 128], replicated
- norm_down: float32 [2, 128], replicated
- w_b: bfloat16 [3, 3, 3, 128, 128], replicated
- norm_b: float32 [3, 2, 128], replicated
Outputs:
- output: bfloat16 [24, 256, 32, 128], P(('pod', 'dp'), 'sp'), parts along dimension 0
There are 2 independent parts. A program takes and returns all parts, laid end to end along the dimension named above; an argument that names none is the same for every part.
All inputs are finite; a program needn't handle non-finite values.
Results may differ from a plain program's by a relative error of at most 0.00451443.
Values are sent between devices in bfloat16 or wider.
A program may use at most 1 GiB of HBM per device.

v0:
```python
import jax
import jax.numpy as jnp
from jax import lax
from jax.sharding import PartitionSpec as P

EPS_VALUE = 1e-5
CONV_DIMS = ('NHWC', 'HWIO', 'NHWC')


def solution(mesh):
    group_size = mesh.shape['sp']
    data_size = mesh.shape['dp']
    to_lower = [(dev_idx, dev_idx + 1) for dev_idx in range(group_size - 1)]
    to_upper = [(dev_idx + 1, dev_idx) for dev_idx in range(group_size - 1)]

    def batch_norm(z_val, norm_pair):
        local_sums = jnp.stack([jnp.sum(z_val, axis=(0, 1, 2)), jnp.sum(z_val * z_val, axis=(0, 1, 2))])
        group_sums = lax.psum(local_sums, ('dp', 'sp'))
        elem_count = z_val.shape[0] * z_val.shape[1] * z_val.shape[2] * data_size * group_size
        mean_val = group_sums[0] / elem_count
        var_val = group_sums[1] / elem_count - mean_val * mean_val
        scaled = norm_pair[0] * (z_val - mean_val) * lax.rsqrt(var_val + EPS_VALUE) + norm_pair[1]
        return jnp.maximum(scaled, 0.0).astype(jnp.bfloat16)

    def same_layer(hidden, weight, norm_pair):
        top_rows = lax.ppermute(hidden[:, -1:], 'sp', to_lower)
        bottom_rows = lax.ppermute(hidden[:, :1], 'sp', to_upper)
        padded = jnp.concatenate([top_rows, hidden, bottom_rows], axis=1)
        z_val = lax.conv_general_dilated(padded, weight, (1, 1), ((0, 0), (1, 1)), dimension_numbers=CONV_DIMS, preferred_element_type=jnp.float32)
        return batch_norm(z_val, norm_pair)

    def down_layer(hidden, weight, norm_pair):
        bottom_rows = lax.ppermute(hidden[:, :1], 'sp', to_upper)
        padded = jnp.concatenate([hidden, bottom_rows], axis=1)
        z_val = lax.conv_general_dilated(padded, weight, (2, 2), ((0, 0), (0, 1)), dimension_numbers=CONV_DIMS, preferred_element_type=jnp.float32)
        return batch_norm(z_val, norm_pair)

    def local_stack(row_tile, w_a, norm_a, w_down, norm_down, w_b, norm_b):
        hidden = row_tile
        for layer_idx in range(w_a.shape[0]):
            hidden = same_layer(hidden, w_a[layer_idx], norm_a[layer_idx])
        hidden = down_layer(hidden, w_down, norm_down)
        for layer_idx in range(w_b.shape[0]):
            hidden = same_layer(hidden, w_b[layer_idx], norm_b[layer_idx])
        return hidden

    act_spec = P(('pod', 'dp'), 'sp', None, None)
    return jax.shard_map(local_stack, mesh=mesh, in_specs=(act_spec, P(), P(), P(), P(), P(), P()), out_specs=act_spec, check_vma=False)
```

profile of v0, /device:TPU:0, one launch (start us, length us, event | category | flops | bytes accessed | tf_op | source)
XLA Modules:
  0.0 364.4 jit_solution(5204684609687147884)
XLA Ops:
  0.0 6.1 %fusion.48 = (bf16[3,1,64,64]{1,3,2,0:T(8,128)(2,1)}, bf16[3,1,64,64]{1,3,2,0:T(8,128)(2,1)S(1)}) fusion(bf16[3,128,64,64]{1,3,2,0:T(8,128)(2,1)} %param.7), kind=kLoop, calls=%fused_computation.108 | loop fusion | bytes 98304 | tf_op jit(solution)/shard_map/slice | solution.py:26
  6.2 3.4 copy.119
  22.0 5.8 %maximum_bitcast_fusion = bf16[130,3,64,64]{0,3,2,1:T(8,128)(2,1)S(1)} fusion(bf16[3,1,64,64]{1,3,2,0:T(8,128)(2,1)} %copy.92, bf16[3,128,64,64]{1,3,2,0:T(8,128)(2,1)S(1)} %copy-done.3, bf16[3,1,64,64]{1,3,2,0:T(8,128)(2,1)} %copy.91), kind=kLoop, calls=%fused_computation.16 | loop fusion | flops 9584640 | bytes 6389760 | tf_op jit(solution)/shard_map/concatenate | solution.py:28
  27.8 5.1 %pad = bf16[130,3,72,64]{0,3,2,1:T(8,128)(2,1)} pad(bf16[130,3,64,64]{0,3,2,1:T(8,128)(2,1)S(1)} %maximum_bitcast_fusion, bf16[]{:T(256)} %constant.22), padding=0_0x0_0x1_7x0_0 | pad | bytes 6789122 | tf_op jit(solution)/shard_map/concatenate | solution.py:28
  32.9 14.3 %copy.94 = bf16[130,3,8,9,64]{4,2,1,3,0:T(8,128)(2,1)} copy(bf16[130,3,8,9,64]{0,4,3,2,1:T(8,128)(2,1)} %bitcast.171) | data formatting | bytes 7188480 | tf_op jit(solution)/shard_map/conv_general_dilated | solution.py:29
  49.1 18.1 %fusion.7 = f32[128,24,9,64]{3,1,2,0:T(8,128)} fusion(bf16[130,3,7,2,64]{4,2,1,3,0:T(8,128)(2,1)S(1)} %slice.169, bf16[130,3,8,9,64]{4,2,1,3,0:T(8,128)(2,1)} %copy.94, bf16[1,3,3,64,64]{4,3,2,1,0:T(8,128)(2,1)S(1)} %copy-done), kind=kOutput, calls=%fused_computation.9 | convolution fusion | flops 2051610624 | bytes 11444736 | tf_op jit(solution)/shard_map/conv_general_dilated | solution.py:29
  67.1 12.8 %copy.95 = f32[128,24,9,64]{0,3,2,1:T(8,128)} copy(f32[128,24,9,64]{3,1,2,0:T(8,128)} %fusion.7) | data formatting | bytes 14155776 | tf_op jit(solution)/shard_map/conv_general_dilated | solution.py:29
  79.9 5.1 %select_reduce_fusion.1 = (f32[64]{0:T(128)S(1)}, f32[64]{0:T(128)S(1)}) fusion(f32[128,24,9,64]{0,3,2,1:T(8,128)} %copy.95, pred[24,9]{1,0:T(8,128)(4,1)S(1)} %copy-done.5), kind=kLoop, calls=%fused_computation.15 | loop fusion | flops 10616704 | bytes 7078616 | tf_op jit(solution)/shard_map/reduce_sum | solution.py:17
  85.0 35.2 %psum.35 = f32[2,64]{1,0:T(2,128)S(1)} all-reduce(f32[2,64]{1,0:T(2,128)S(1)} %pad_maximum_fusion), channel_id=1, replica_groups=mesh['pod'=2,'dp'=4,'sp'=4] {'dp','sp'}, use_global_device_ids=true, to_apply=%region_2.0 | all-reduce | flops 128 | bytes 1024 | tf_op jit(solution)/shard_map/psum | solution.py:18
  120.2 9.3 %maximum_convert_fusion = bf16[128,24,9,64]{0,3,2,1:T(8,128)(2,1)S(1)} fusion(f32[128,24,9,64]{0,3,2,1:T(8,128)} %copy.95, f32[64]{0:T(128)S(1)} %get-tuple-element.32, f32[64]{0:T(128)S(1)} %fusion.44, f32[64]{0:T(128)S(1)} %get-tuple-element.31, f32[64]{0:T(128)S(1)} %multiply_bitcast_fusion.4, pred[24,9]{1,0:T(8,128)(4,1)S(1)} %copy-done.5), kind=kLoop, calls=%fused_computation.13 | loop fusion | flops 12386304 | bytes 10618072 | tf_op jit(solution)/shard_map/convert_element_type | solution.py:23
  140.5 7.0 %maximum_bitcast_fusion.1 = bf16[129,3,64,64]{0,3,2,1:T(8,128)(2,1)} fusion(bf16[3,1,64,64]{1,3,2,0:T(8,128)(2,1)} %copy.97, bf16[3,128,64,64]{1,3,2,0:T(8,128)(2,1)S(1)} %slice_bitcast_fusion), kind=kLoop, calls=%fused_computation.17 | loop fusion | flops 6340608 | bytes 6340608 | tf_op jit(solution)/shard_map/concatenate | solution.py:34
  147.4 4.6 %pad.2 = bf16[129,3,80,64]{0,3,2,1:T(8,128)(2,1)S(1)} pad(bf16[129,3,64,64]{0,3,2,1:T(8,128)(2,1)} %maximum_bitcast_fusion.1, bf16[]{:T(256)} %constant.22), padding=0_0x0_0x0_16x0_0 | pad | bytes 7133186 | tf_op jit(solution)/shard_map/concatenate | solution.py:34
  152.2 5.2 %fusion.4 = bf16[129,3,8,12,64]{0,4,3,2,1:T(8,128)(2,1)} fusion(bf16[129,3,7,2,64]{0,4,3,2,1:T(8,128)(2,1)S(1)} %slice.173, bf16[129,3,8,10,64]{0,4,3,2,1:T(8,128)(2,1)S(1)} %bitcast.169), kind=kLoop, calls=%fused_computation.6 | loop fusion | flops 14266368 | bytes 9411840 | tf_op jit(solution)/shard_map/conv_general_dilated | solution.py:35
  157.4 17.1 %copy.98 = bf16[129,3,8,12,64]{4,2,1,3,0:T(8,128)(2,1)} copy(bf16[129,3,8,12,64]{0,4,3,2,1:T(8,128)(2,1)} %fusion.4) | data formatting | bytes 9510912 | tf_op jit(solution)/shard_map/conv_general_dilated | solution.py:35
  174.5 8.1 %select_reduce_fusion.9 = (f32[128]{0:T(128)S(1)}, f32[128]{0:T(128)S(1)}, f32[64,24,5,128]{3,1,2,0:T(8,128)}) fusion(pred[24,5]{0,1:T(8,128)(4,1)S(1)} %copy-done.4, bf16[3,3,64,128]{3,2,1,0:T(8,128)(2,1)S(1)} %copy-done.10, bf16[129,3,8,12,64]{4,2,1,3,0:T(8,128)(2,1)} %copy.98), kind=kOutput, calls=%fused_computation.34 | convolution fusion | flops 1138360064 | bytes 8836216 | tf_op jit(solution)/shard_map/conv_general_dilated | solution.py:35
  182.6 30.6 %psum.36 = f32[2,128]{1,0:T(2,128)S(1)} all-reduce(f32[2,128]{1,0:T(2,128)S(1)} %pad_maximum_fusion.1), channel_id=1, replica_groups=mesh['pod'=2,'dp'=4,'sp'=4] {'dp','sp'}, use_global_device_ids=true, to_apply=%region_5.0 | all-reduce | flops 256 | bytes 2048 | tf_op jit(solution)/shard_map/psum | solution.py:18
  218.3 3.2 collective-permute-start.3
  224.7 7.2 %select_reduce_fusion.7 = (f32[128]{0:T(128)S(1)}, f32[128]{0:T(128)S(1)}, f32[64,24,5,128]{3,1,2,0:T(8,128)}) fusion(pred[24,5]{0,1:T(8,128)(4,1)S(1)} %copy-done.4, bf16[3,3,3,128,128]{4,3,2,1,0:T(8,128)(2,1)S(1)} %copy-done.9, bf16[66,3,8,7,128]{4,0,3,2,1:T(8,128)(2,1)S(1)} %fusion.16), kind=kOutput, calls=%fused_computation.31 | convolution fusion | flops 2270822400 | bytes 7325696 | tf_op jit(solution)/shard_map/conv_general_dilated | solution.py:29
  231.9 29.8 %psum.37 = f32[2,128]{1,0:T(2,128)S(1)} all-reduce(f32[2,128]{1,0:T(2,128)S(1)} %pad_maximum_fusion.2), channel_id=1, replica_groups=mesh['pod'=2,'dp'=4,'sp'=4] {'dp','sp'}, use_global_device_ids=true, to_apply=%region_8.0 | all-reduce | flops 256 | bytes 2048 | tf_op jit(solution)/shard_map/psum | solution.py:18
  266.9 3.4 collective-permute-start.5
  272.7 7.2 %select_reduce_fusion.5 = (f32[128]{0:T(128)S(1)}, f32[128]{0:T(128)S(1)}, f32[64,24,5,128]{3,1,2,0:T(8,128)}) fusion(pred[24,5]{0,1:T(8,128)(4,1)S(1)} %copy-done.4, bf16[3,3,3,128,128]{4,3,2,1,0:T(8,128)(2,1)S(1)} %copy-done.9, bf16[66,3,8,7,128]{4,0,3,2,1:T(8,128)(2,1)S(1)} %fusion.17), kind=kOutput, calls=%fused_computation.28 | convolution fusion | flops 2270822400 | bytes 7325696 | tf_op jit(solution)/shard_map/conv_general_dilated | solution.py:29
  279.9 30.3 %psum.38 = f32[2,128]{1,0:T(2,128)S(1)} all-reduce(f32[2,128]{1,0:T(2,128)S(1)} %pad_maximum_fusion.3), channel_id=1, replica_groups=mesh['pod'=2,'dp'=4,'sp'=4] {'dp','sp'}, use_global_device_ids=true, to_apply=%region_11.0 | all-reduce | flops 256 | bytes 2048 | tf_op jit(solution)/shard_map/psum | solution.py:18
  321.2 7.2 %select_reduce_fusion.3 = (f32[128]{0:T(128)S(1)}, f32[128]{0:T(128)S(1)}, f32[64,24,5,128]{3,1,2,0:T(8,128)}) fusion(pred[24,5]{0,1:T(8,128)(4,1)S(1)} %copy-done.4, bf16[3,3,3,128,128]{4,3,2,1,0:T(8,128)(2,1)S(1)} %copy-done.9, bf16[66,3,8,7,128]{4,0,3,2,1:T(8,128)(2,1)S(1)} %fusion.18), kind=kOutput, calls=%fused_computation.25 | convolution fusion | flops 2270822400 | bytes 7325696 | tf_op jit(solution)/shard_map/conv_general_dilated | solution.py:29
  328.4 29.8 %psum.39 = f32[2,128]{1,0:T(2,128)S(1)} all-reduce(f32[2,128]{1,0:T(2,128)S(1)} %pad_maximum_fusion.4), channel_id=1, replica_groups=mesh['pod'=2,'dp'=4,'sp'=4] {'dp','sp'}, use_global_device_ids=true, to_apply=%region_14.0 | all-reduce | flops 256 | bytes 2048 | tf_op jit(solution)/shard_map/psum | solution.py:18
  (118 shorter events, 57.7 us)
Async XLA Ops:
  0.0 49.1 %copy-start = (bf16[1,3,3,64,64]{4,3,2,1,0:T(8,128)(2,1)S(1)}, bf16[1,3,3,64,64]{4,3,2,1,0:T(8,128)(2,1)}, u32[]{:S(2)}) copy-start(bf16[1,3,3,64,64]{4,3,2,1,0:T(8,128)(2,1)} %param.8) | copy-start | bytes 221188
  6.2 9.3 %copy-start.7 = (f32[1,2,64]{2,1,0:T(2,128)S(1)}, f32[1,2,64]{2,1,0:T(2,128)}, u32[]{:S(2)}) copy-start(f32[1,2,64]{2,1,0:T(2,128)} %param.9) | copy-start | bytes 1540
  6.2 9.3 %copy-start.6 = (f32[3,2,128]{2,1,0:T(2,128)S(1)}, f32[3,2,128]{2,1,0:T(2,128)}, u32[]{:S(2)}) copy-start(f32[3,2,128]{2,1,0:T(2,128)} %param.13) | copy-start | bytes 9220
  6.2 9.3 %copy-start.8 = (f32[2,128]{1,0:T(2,128)S(1)}, f32[2,128]{1,0:T(2,128)}, u32[]{:S(2)}) copy-start(f32[2,128]{1,0:T(2,128)} %param.11) | copy-start | bytes 3076
  9.6 6.0 %collective-permute-start = (bf16[3,1,64,64]{3,2,1,0:T(8,128)(2,1)S(1)}, bf16[3,1,64,64]{3,2,1,0:T(8,128)(2,1)S(1)}, u32[]{:S(2)}, u32[]{:S(2)}) collective-permute-start(bf16[3,1,64,64]{3,2,1,0:T(8,128)(2,1)S(1)} %copy.119), channel_id=1, source_target_pairs={{0,1},{1,2},{2,3},{4,5},{5,6},{6,7},{8,9},{9,10},{10,11},{12,13},{... | collective-permute-start | bytes 73736 | tf_op jit(solution)/shard_map/ppermute | solution.py:26
  13.6 8.5 %copy-start.3 = (bf16[3,128,64,64]{1,3,2,0:T(8,128)(2,1)S(1)}, bf16[3,128,64,64]{1,3,2,0:T(8,128)(2,1)}, u32[]{:S(2)}) copy-start(bf16[3,128,64,64]{1,3,2,0:T(8,128)(2,1)} %param.7) | copy-start | bytes 9437188
  13.6 5.5 %collective-permute-start.1 = (bf16[3,1,64,64]{3,2,1,0:T(8,128)(2,1)S(1)}, bf16[3,1,64,64]{3,2,1,0:T(8,128)(2,1)S(1)}, u32[]{:S(2)}, u32[]{:S(2)}) collective-permute-start(bf16[3,1,64,64]{3,2,1,0:T(8,128)(2,1)S(1)} %copy.120), channel_id=1, source_target_pairs={{1,0},{2,1},{3,2},{5,4},{6,5},{7,6},{9,8},{10,9},{11,10},{13,12},{... | collective-permute-start | bytes 73736 | tf_op jit(solution)/shard_map/ppermute | solution.py:27
  67.1 12.8 %copy-start.5 = (pred[24,9]{1,0:T(8,128)(4,1)S(1)}, pred[24,9]{1,0:T(8,128)(4,1)}, u32[]{:S(2)}) copy-start(pred[24,9]{1,0:T(8,128)(4,1)} %constant.56) | copy-start | bytes 652
  129.5 1.8 copy-start.2
  133.3 3.9 %collective-permute-start.2 = (bf16[3,1,64,64]{3,2,1,0:T(8,128)(2,1)S(1)}, bf16[3,1,64,64]{3,2,1,0:T(8,128)(2,1)S(1)}, u32[]{:S(2)}, u32[]{:S(2)}) collective-permute-start(bf16[3,1,64,64]{3,2,1,0:T(8,128)(2,1)S(1)} %slice_bitcast_fusion.5), channel_id=1, source_target_pairs={{1,0},{2,1},{3,2},{5,4},{6,5},{7,6},{9,8},{10,9},{11,10},{13,12},{... | collective-permute-start | bytes 73736 | tf_op jit(solution)/shard_map/ppermute | solution.py:33
  157.4 17.1 %copy-start.4 = (pred[24,5]{0,1:T(8,128)(4,1)S(1)}, pred[24,5]{0,1:T(8,128)(4,1)}, u32[]{:S(2)}) copy-start(pred[24,5]{0,1:T(8,128)(4,1)} %constant.52) | copy-start | bytes 364
  157.4 17.1 %copy-start.10 = (bf16[3,3,64,128]{3,2,1,0:T(8,128)(2,1)S(1)}, bf16[3,3,64,128]{3,2,1,0:T(8,128)(2,1)}, u32[]{:S(2)}) copy-start(bf16[3,3,64,128]{3,2,1,0:T(8,128)(2,1)} %param.10) | copy-start | bytes 442372
  216.9 5.3 %collective-permute-start.4 = (bf16[3,1,32,128]{3,1,2,0:T(2,128)(2,1)S(1)}, bf16[3,1,32,128]{3,1,2,0:T(2,128)(2,1)S(1)}, u32[]{:S(2)}, u32[]{:S(2)}) collective-permute-start(bf16[3,1,32,128]{3,1,2,0:T(2,128)(2,1)S(1)} %copy.102), channel_id=1, source_target_pairs={{1,0},{2,1},{3,2},{5,4},{6,5},{7,6},{9,8},{10,9},{11,10},{13,12},{... | collective-permute-start | bytes 73736 | tf_op jit(solution)/shard_map/ppermute | solution.py:27
  218.3 3.9 %collective-permute-start.3 = (bf16[3,1,32,128]{3,2,0,1:T(8,128)(2,1)S(1)}, bf16[3,1,32,128]{3,2,0,1:T(8,128)(2,1)S(1)}, u32[]{:S(2)}, u32[]{:S(2)}) collective-permute-start(bf16[3,1,32,128]{3,2,0,1:T(8,128)(2,1)S(1)} %slice_bitcast_fusion.11), channel_id=1, source_target_pairs={{0,1},{1,2},{2,3},{4,5},{5,6},{6,7},{8,9},{9,10},{10,11},{12,13},{... | collective-permute-start | bytes 73736 | tf_op jit(solution)/shard_map/ppermute | solution.py:26
  223.5 1.2 copy-start.9
  265.5 5.3 %collective-permute-start.6 = (bf16[3,1,32,128]{3,1,2,0:T(2,128)(2,1)S(1)}, bf16[3,1,32,128]{3,1,2,0:T(2,128)(2,1)S(1)}, u32[]{:S(2)}, u32[]{:S(2)}) collective-permute-start(bf16[3,1,32,128]{3,1,2,0:T(2,128)(2,1)S(1)} %copy.108), channel_id=1, source_target_pairs={{1,0},{2,1},{3,2},{5,4},{6,5},{7,6},{9,8},{10,9},{11,10},{13,12},{... | collective-permute-start | bytes 73736 | tf_op jit(solution)/shard_map/ppermute | solution.py:27
  266.9 3.9 %collective-permute-start.5 = (bf16[3,1,32,128]{3,2,0,1:T(8,128)(2,1)S(1)}, bf16[3,1,32,128]{3,2,0,1:T(8,128)(2,1)S(1)}, u32[]{:S(2)}, u32[]{:S(2)}) collective-permute-start(bf16[3,1,32,128]{3,2,0,1:T(8,128)(2,1)S(1)} %slice_bitcast_fusion.9), channel_id=1, source_target_pairs={{0,1},{1,2},{2,3},{4,5},{5,6},{6,7},{8,9},{9,10},{10,11},{12,13},{... | collective-permute-start | bytes 73736 | tf_op jit(solution)/shard_map/ppermute | solution.py:26
  314.0 5.3 %collective-permute-start.8 = (bf16[3,1,32,128]{3,1,2,0:T(2,128)(2,1)S(1)}, bf16[3,1,32,128]{3,1,2,0:T(2,128)(2,1)S(1)}, u32[]{:S(2)}, u32[]{:S(2)}) collective-permute-start(bf16[3,1,32,128]{3,1,2,0:T(2,128)(2,1)S(1)} %copy.114), channel_id=1, source_target_pairs={{1,0},{2,1},{3,2},{5,4},{6,5},{7,6},{9,8},{10,9},{11,10},{13,12},{... | collective-permute-start | bytes 73736 | tf_op jit(solution)/shard_map/ppermute | solution.py:27
  315.4 3.9 %collective-permute-start.7 = (bf16[3,1,32,128]{3,2,0,1:T(8,128)(2,1)S(1)}, bf16[3,1,32,128]{3,2,0,1:T(8,128)(2,1)S(1)}, u32[]{:S(2)}, u32[]{:S(2)}) collective-permute-start(bf16[3,1,32,128]{3,2,0,1:T(8,128)(2,1)S(1)} %slice_bitcast_fusion.7), channel_id=1, source_target_pairs={{0,1},{1,2},{2,3},{4,5},{5,6},{6,7},{8,9},{9,10},{10,11},{12,13},{... | collective-permute-start | bytes 73736 | tf_op jit(solution)/shard_map/ppermute | solution.py:26
  361.4 2.8 copy-start.1
where the time goes:
time: 369 us; the launch traced here: 364 us
  blocking collectives  156 us (42%)
  local copies, waits for them, and re-layouts  89 us (24%)
  other arithmetic  49.9 us (14%)
  matrix products  47.7 us (13%)
  starting transfers between devices  19.3 us (5%)
    psum x5, blocking collectives, batch_norm(): group_sums = lax.psum(local_sums, ('dp', 'sp'))  156 us
    conv_general_dilated x4, matrix products, same_layer(): lax.conv_general_dilated(padded, weight, (1, 1), ((0, 0), (1, 1)), dimens...  39.6 us
    conv_general_dilated x6, local copies, waits for them, and re-layouts, same_layer(): lax.conv_general_dilated(padded, weight, (1, 1), ((0, 0), (1, 1)), dimens...  29.1 us
    convert_element_type x5, other arithmetic, batch_norm(): return jnp.maximum(scaled, 0.0).astype(jnp.bfloat16)  21.7 us
    conv_general_dilated x2, local copies, waits for them, and re-layouts, down_layer(): lax.conv_general_dilated(padded, weight, (2, 2), ((0, 0), (0, 1)), dimens...  17.2 us
    ppermute x4, starting transfers between devices, same_layer(): top_rows = lax.ppermute(hidden[:, -1:], 'sp', to_lower)  12.3 us
    convert_element_type x27, local copies, waits for them, and re-layouts, batch_norm(): return jnp.maximum(scaled, 0.0).astype(jnp.bfloat16)  9.51 us
    concatenate x4, other arithmetic, same_layer(): padded = jnp.concatenate([top_rows, hidden, bottom_rows], axis=1)  9.13 us
  transfers between devices with their start and end apart: 9, of which 4 were waited for; matrix products, arithmetic and copies ran while one was open for 2% of the time, Pallas kernels for 0%

commit v1 on v0

v1 whole, which is shorter than its diff:
```python
import functools

import jax
import jax.numpy as jnp
from jax import lax
from jax.experimental import pallas as pl
from jax.experimental.pallas import tpu as pltpu
from jax.sharding import PartitionSpec as P

EPS_VALUE = 1e-5
F32 = jnp.float32
BF16 = jnp.bfloat16
NB = 3
MESH = pl.DeviceIdType.MESH


def fused_kernel(dp_size, sp_size, img, wa, na, wd, nd, wb, nb, out,
                 xv, t32, pa, za, sa, sh, zb, yb, wam, wdm, wbm,
                 wav, nav, wdv, ndv, wbv, nbv, st, o32, ov,
                 img_sem, w_sem, st_send, st_recv, halo_send, halo_recv, out_sem):
    group = dp_size * sp_size
    pod = lax.axis_index("pod")
    dp = lax.axis_index("dp")
    sp = lax.axis_index("sp")
    me = dp * sp_size + sp
    is_top = sp == 0
    is_bottom = sp == sp_size - 1

    def peer_id(k):
        peer = lax.rem(me + k, group)
        return (pod, lax.div(peer, sp_size), lax.rem(peer, sp_size))

    barrier = pltpu.get_barrier_semaphore()
    for k in range(1, group):
        pl.semaphore_signal(barrier, inc=1, device_id=peer_id(k), device_id_type=MESH)

    img_copies = [pltpu.make_async_copy(img.at[n], xv.at[n, pl.ds(64, 4096)], img_sem.at[n]) for n in range(NB)]
    for copy in img_copies:
        copy.start()
    w_copies = [pltpu.make_async_copy(src, dst, w_sem.at[i]) for i, (src, dst) in enumerate(
        [(wa, wav), (na, nav), (wd, wdv), (nd, ndv), (wb, wbv), (nb, nbv)])]
    for copy in w_copies:
        copy.start()

    for n in range(NB):
        xv[n, 0:64] = jnp.zeros((64, 128), BF16)
        xv[n, 4160:4224] = jnp.zeros((64, 128), BF16)
        sa[0, n, 16, 0] = jnp.zeros((64, 128), BF16)
        sh[n, 16, 0] = jnp.zeros((64, 128), BF16)
        for p in range(3):
            yb[p, n, 0, 0] = jnp.zeros((64, 128), BF16)
            yb[p, n, 16, 1] = jnp.zeros((64, 128), BF16)

    @pl.when(is_top)
    def _():
        t32[:, :, 7:8, :] = jnp.zeros((NB, 33, 1, 128), F32)
        zb[:, :, :, :, 7:8, :] = jnp.zeros((2, 2, NB, 16, 1, 128), F32)

    @pl.when(is_bottom)
    def _():
        t32[:, :, 136:137, :] = jnp.zeros((NB, 33, 1, 128), F32)
        za[:, :, :, 64:65, :] = jnp.zeros((2, NB, 32, 1, 128), F32)
        zb[:, :, :, :, 72:73, :] = jnp.zeros((2, 2, NB, 16, 1, 128), F32)

    for copy in w_copies:
        copy.wait()

    zero64 = jnp.zeros((64, 64), BF16)
    for t in range(4):
        for u in range(4):
            parts = []
            for cp in range(2):
                for rp in range(2):
                    p, q = t - rp, u - cp
                    ok = 0 <= p <= 2 and 0 <= q <= 2
                    parts.append(wav[0, p, q] if ok else zero64)
            row = t * 256 + u * 64
            wam[row:row + 64, :] = jnp.concatenate(parts, axis=1)

    def down_tap(v, p):
        cols = []
        for jp in range(2):
            q = v - 2 * jp
            cols.append(wdv[p, q] if 0 <= q <= 2 else jnp.zeros((64, 128), BF16))
        return jnp.concatenate(cols, axis=1)

    for v in range(5):
        for rp in range(2):
            wdm[v * 128 + rp * 64:v * 128 + rp * 64 + 64, :] = down_tap(v, rp)
    for v in range(6):
        wdm[640 + v * 64:640 + v * 64 + 64, :] = down_tap(v, 2)

    for layer in range(3):
        for p in range(3):
            for u in range(4):
                for jp in range(2):
                    q = u - jp
                    blk = wbv[layer, p, q] if 0 <= q <= 2 else jnp.zeros((128, 128), BF16)
                    row = (p * 4 + u) * 128
                    wbm[layer, row:row + 128, jp * 128:jp * 128 + 128] = blk

    for n in range(NB):
        img_copies[n].wait()

        def to_rows(a, carry, n=n):
            tile = xv[n, pl.ds(pl.multiple_of(a * 128, 128), 128), :]
            t32[n, a, 8:136, :] = tile.T.astype(F32)
            return carry
        lax.fori_loop(0, 33, to_rows, 0)

    pl.semaphore_wait(barrier, group - 1)

    def exchange(idx, top_src, bottom_src, top_dst, bottom_dst):
        up = pltpu.make_async_remote_copy(top_src, bottom_dst, halo_send.at[idx, 0], halo_recv.at[idx, 0],
                                          device_id=(pod, dp, lax.rem(sp + sp_size - 1, sp_size)), device_id_type=MESH)
        down = None
        if bottom_src is not None:
            down = pltpu.make_async_remote_copy(bottom_src, top_dst, halo_send.at[idx, 1], halo_recv.at[idx, 1],
                                                device_id=(pod, dp, lax.rem(sp + 1, sp_size)), device_id_type=MESH)

        def start():
            @pl.when(sp > 0)
            def _():
                up.start()
            if down is not None:
                @pl.when(sp < sp_size - 1)
                def _():
                    down.start()

        def wait():
            @pl.when(sp > 0)
            def _():
                up.wait_send()
                if down is not None:
                    down.wait_recv()

            @pl.when(sp < sp_size - 1)
            def _():
                up.wait_recv()
                if down is not None:
                    down.wait_send()
        return start, wait

    start, wait = exchange(0, t32.at[:, :, pl.ds(8, 1), :], t32.at[:, :, pl.ds(135, 1), :],
                           t32.at[:, :, pl.ds(7, 1), :], t32.at[:, :, pl.ds(136, 1), :])
    start()

    def split_rows(taps):
        def body(a, carry):
            for n in range(NB):
                for t in taps:
                    pa[t, n, a] = t32[n, a, pl.ds(7 + t, 64, stride=2), :].astype(BF16)
            return carry
        lax.fori_loop(0, 33, body, 0)

    split_rows((1, 2))
    wait()
    split_rows((0, 3))

    def sums(z_val, carry):
        s1, s2 = carry
        z8 = z_val.reshape(64, 8, 256)
        return s1 + jnp.sum(z8, axis=0), s2 + jnp.sum(z8 * z8, axis=0)

    zero_sums = (jnp.zeros((8, 256), F32), jnp.zeros((8, 256), F32))

    def send_sums(layer, carry):
        rows = []
        for s in carry:
            r = jnp.sum(s, axis=0, keepdims=True)
            rows.append(r[:, :128] + r[:, 128:])
        st[layer, me] = jnp.concatenate(rows, axis=0)
        for k in range(1, group):
            pltpu.make_async_remote_copy(st.at[layer, me], st.at[layer, me], st_send.at[layer], st_recv.at[layer],
                                         device_id=peer_id(k), device_id_type=MESH).start()

    def recv_sums(layer, gamma, beta, count, fold):
        others = st.at[layer, pl.ds(0, group - 1)]
        pltpu.make_async_copy(others, others, st_recv.at[layer]).wait()
        pltpu.make_async_copy(others, others, st_send.at[layer]).wait()
        total = jnp.sum(st[layer], axis=0)
        if fold:
            total = total + pltpu.roll(total, 64, 1)
        mean = total[0:1] / count
        var = total[1:2] / count - mean * mean
        scale = gamma * lax.rsqrt(var + EPS_VALUE)
        return scale, beta - mean * scale

    def conv_a(it, carry):
        n = lax.div(it, 4)
        a0 = lax.rem(it, 4) * 8
        parts = []
        for t in range(4):
            parts.append(pa[t, n, pl.ds(a0, 8)].reshape(512, 128))
            parts.append(pa[t, n, pl.ds(a0 + 1, 8)].reshape(512, 128))
        z_val = jnp.dot(jnp.concatenate(parts, axis=1), wam[...], preferred_element_type=F32)
        for cp in range(2):
            za[cp, n, pl.ds(a0, 8), 0:64, :] = z_val[:, cp * 128:cp * 128 + 128].reshape(8, 64, 128)
        return sums(z_val, carry)

    carry = lax.fori_loop(0, NB * 4, conv_a, zero_sums)
    send_sums(0, carry)
    start, wait = exchange(1, za.at[:, :, :, pl.ds(0, 1), :], None, None, za.at[:, :, :, pl.ds(64, 1), :])
    start()
    pixels = float(NB * 128 * 64 * group)
    gamma = jnp.concatenate([nav[0, 0:1, :]] * 2, axis=1)
    beta = jnp.concatenate([nav[0, 1:2, :]] * 2, axis=1)
    scale, shift = recv_sums(0, gamma, beta, pixels, True)
    wait()

    row_idx = lax.broadcasted_iota(jnp.int32, (64, 128), 0)
    lane_idx = lax.broadcasted_iota(jnp.int32, (64, 128), 1)
    low_lanes = lane_idx < 64
    cut_top = jnp.logical_and(row_idx == 0, is_top)
    cut_bottom = jnp.logical_and(row_idx == 63, is_bottom)

    def norm_a(it, carry):
        n = lax.div(it, 16)
        g = lax.rem(it, 16)
        for b in range(2):
            a = g * 2 + b
            for cp in range(2):
                y = jnp.maximum(za[cp, n, a, 0:64, :] * scale + shift, 0.0)
                sa[cp, n, g, b] = y.astype(BF16)
            z_next = jnp.where(low_lanes, za[0, n, a, 1:65, :], pltpu.roll(za[1, n, a, 1:65, :], 64, 1))
            y = jnp.maximum(z_next * scale + shift, 0.0)
            sh[n, g, b] = jnp.where(cut_bottom, 0.0, y).astype(BF16)
        return carry
    lax.fori_loop(0, NB * 16, norm_a, 0)

    def store_z(par, n, g0, z_val):
        for jp in range(2):
            zb[par, jp, n, pl.ds(g0, 8), 8:72, :] = z_val[:, jp * 128:jp * 128 + 128].reshape(8, 64, 128)

    def conv_down(it, carry):
        n = lax.div(it, 2)
        g0 = lax.rem(it, 2) * 8
        here, next_ = pl.ds(g0, 8), pl.ds(g0 + 1, 8)
        parts = [sa[0, n, here, 0], sa[1, n, here, 0], sa[0, n, here, 1], sa[1, n, here, 1], sa[0, n, next_, 0],
                 sh[n, here, 0], sh[n, here, 1], sh[n, next_, 0]]
        lhs = jnp.concatenate([x.reshape(512, 128) for x in parts], axis=1)
        z_val = jnp.dot(lhs, wdm[...], preferred_element_type=F32)
        store_z(0, n, g0, z_val)
        return sums(z_val, carry)

    def finish(layer, par, carry, gamma, beta, count, halo):
        send_sums(layer, carry)
        if halo:
            start, wait = exchange(layer + 1, zb.at[par, :, :, :, pl.ds(8, 1), :], zb.at[par, :, :, :, pl.ds(71, 1), :],
                                   zb.at[par, :, :, :, pl.ds(7, 1), :], zb.at[par, :, :, :, pl.ds(72, 1), :])
            start()
        scale, shift = recv_sums(layer, gamma, beta, count, False)
        if halo:
            wait()
        return scale, shift

    carry = lax.fori_loop(0, NB * 2, conv_down, zero_sums)
    pixels = float(NB * 64 * 32 * group)
    scale, shift = finish(1, 0, carry, ndv[0:1], ndv[1:2], pixels, True)

    for layer in range(3):
        par = layer % 2

        def norm_b(it, carry, par=par, scale=scale, shift=shift):
            n = lax.div(it, 16)
            g = lax.rem(it, 16)
            for jp in range(2):
                for p in range(3):
                    y = jnp.maximum(zb[par, jp, n, g, 7 + p:71 + p, :] * scale + shift, 0.0)
                    if p == 0:
                        y = jnp.where(cut_top, 0.0, y)
                    if p == 2:
                        y = jnp.where(cut_bottom, 0.0, y)
                    yb[p, n, g + jp, 1 - jp] = y.astype(BF16)
            return carry
        lax.fori_loop(0, NB * 16, norm_b, 0)

        def conv_b(it, carry, layer=layer, par=par):
            n = lax.div(it, 2)
            g0 = lax.rem(it, 2) * 8
            parts = []
            for p in range(3):
                for u in range(4):
                    parts.append(yb[p, n, pl.ds(g0 + u // 2, 8), u % 2].reshape(512, 128))
            z_val = jnp.dot(jnp.concatenate(parts, axis=1), wbm[layer], preferred_element_type=F32)
            store_z(1 - par, n, g0, z_val)
            return sums(z_val, carry)
        carry = lax.fori_loop(0, NB * 2, conv_b, zero_sums)
        scale, shift = finish(layer + 2, 1 - par, carry, nbv[layer, 0:1], nbv[layer, 1:2], pixels, layer < 2)

    out_copies = []
    for n in range(NB):
        def norm_out(g, carry, n=n):
            for jp in range(2):
                y = jnp.maximum(zb[1, jp, n, g, 8:72, :] * scale + shift, 0.0)
                o32[n, pl.ds(g * 2 + jp, 64, stride=33), :] = y
            return carry
        lax.fori_loop(0, 16, norm_out, 0)

        def pack_out(i, carry, n=n):
            ov[n, i] = o32[n, pl.ds(i * 33, 32), :].astype(BF16)
            return carry
        lax.fori_loop(0, 64, pack_out, 0)
        copy = pltpu.make_async_copy(ov.at[n], out.at[n], out_sem.at[n])
        copy.start()
        out_copies.append(copy)
    for copy in out_copies:
        copy.wait()


def solution(mesh):
    dp_size, sp_size = mesh.shape["dp"], mesh.shape["sp"]
    group = dp_size * sp_size

    def body(images, w_a, norm_a, w_down, norm_down, w_b, norm_b):
        img = jnp.transpose(images, (0, 2, 3, 1)).reshape(NB, 4096, 128)
        vm = pltpu.VMEM
        any_spec = pl.BlockSpec(memory_space=pl.ANY)
        return pl.pallas_call(
            functools.partial(fused_kernel, dp_size, sp_size),
            out_shape=jax.ShapeDtypeStruct((NB, 64, 32, 128), BF16),
            in_specs=[any_spec] * 7,
            out_specs=any_spec,
            scratch_shapes=[
                vm((NB, 4224, 128), BF16),
                vm((NB, 33, 144, 128), F32),
                vm((4, NB, 33, 64, 128), BF16),
                vm((2, NB, 32, 72, 128), F32),
                vm((2, NB, 17, 2, 64, 128), BF16),
                vm((NB, 17, 2, 64, 128), BF16),
                vm((2, 2, NB, 16, 80, 128), F32),
                vm((3, NB, 17, 2, 64, 128), BF16),
                vm((1024, 256), BF16),
                vm((1024, 256), BF16),
                vm((3, 1536, 256), BF16),
                vm((1, 3, 3, 64, 64), BF16),
                vm((1, 2, 64), F32),
                vm((3, 3, 64, 128), BF16),
                vm((2, 128), F32),
                vm((3, 3, 3, 128, 128), BF16),
                vm((3, 2, 128), F32),
                vm((5, group, 2, 128), F32),
                vm((NB, 64 * 33, 128), F32),
                vm((NB, 64, 32, 128), BF16),
                pltpu.SemaphoreType.DMA((NB,)),
                pltpu.SemaphoreType.DMA((6,)),
                pltpu.SemaphoreType.DMA((5,)),
                pltpu.SemaphoreType.DMA((5,)),
                pltpu.SemaphoreType.DMA((5, 2)),
                pltpu.SemaphoreType.DMA((5, 2)),
                pltpu.SemaphoreType.DMA((NB,)),
            ],
            compiler_params=pltpu.CompilerParams(
                collective_id=0, has_side_effects=True, vmem_limit_bytes=62 * 1024 * 1024),
        )(img, w_a, norm_a, w_down, norm_down, w_b, norm_b)

    act_spec = P(("pod", "dp"), "sp", None, None)
    return jax.shard_map(body, mesh=mesh, in_specs=(act_spec, P(), P(), P(), P(), P(), P()), out_specs=act_spec, check_vma=False)
```

time: 369 us -> 69.5 us (0.19); the launches traced: 364 us -> 69.3 us
  blocking collectives: 156 us -> 0 us
  local copies, waits for them, and re-layouts: 89 us -> 2.86 us
  Pallas kernels: 0 us -> 66.5 us
  other arithmetic: 49.9 us -> 0 us
  matrix products: 47.7 us -> 0 us
  starting transfers between devices: 19.3 us -> 0 us
    psum x5 -> x0, blocking collectives: 156 us -> none  [batch_norm(): group_sums = lax.psum(local_sums, ('dp', 'sp'))]
    pallas_call x0 -> x1, Pallas kernels: none -> 66.5 us  [body(): pl.pallas_call(functools.partial(fused_kernel, dp_size, sp_size), out_sha...]
    conv_general_dilated x5 -> x0, matrix products: 47.7 us -> none  [the longest x4 39.6 us: same_layer(): lax.conv_general_dilated(padded, weight, (1, 1), ((0, 0), (1, 1)), dimens...]
    conv_general_dilated x8 -> x0, local copies, waits for them, and re-layouts: 46.3 us -> none  [the longest x6 29.1 us: same_layer(): lax.conv_general_dilated(padded, weight, (1, 1), ((0, 0), (1, 1)), dimens...]
    convert_element_type x5 -> x0, other arithmetic: 21.7 us -> none  [batch_norm(): return jnp.maximum(scaled, 0.0).astype(jnp.bfloat16)]
    ppermute x9 -> x0, starting transfers between devices: 19.3 us -> none  [the longest x4 12.3 us: same_layer(): top_rows = lax.ppermute(hidden[:, -1:], 'sp', to_lower)]
    concatenate x5 -> x0, other arithmetic: 16.1 us -> none  [the longest x4 9.13 us: same_layer(): padded = jnp.concatenate([top_rows, hidden, bottom_rows], axis=1)]
    concatenate x5 -> x0, local copies, waits for them, and re-layouts: 10.3 us -> none  [the longest x4 5.68 us: same_layer(): padded = jnp.concatenate([top_rows, hidden, bottom_rows], axis=1)]
  transfers between devices with their start and end apart: 9 -> 0, of which waited for: 4 -> 0; matrix products, arithmetic and copies ran while one was open for 2% -> 0% of each run, Pallas kernels for 0% -> 0%
where the time goes in v1:
time: 69.5 us; the launch traced here: 69.3 us
  Pallas kernels  66.5 us (96%)
  local copies, waits for them, and re-layouts  2.86 us (4%)
    pallas_call x1, Pallas kernels, body(): pl.pallas_call(functools.partial(fused_kernel, dp_size, sp_size), out_sha...  66.5 us
    unnamed x1, local copies, waits for them, and re-layouts  2.86 us

profile of v1, /device:TPU:0, one launch (start us, length us, event | category | flops | bytes accessed | tf_op | source)
XLA Modules:
  0.0 69.3 jit_solution(3709284617840761769)
XLA Ops:
  0.0 66.5 %shard_map.73 = bf16[3,64,32,128]{3,2,1,0:T(8,128)(2,1)} custom-call(bf16[3,4096,128]{2,1,0:T(8,128)(2,1)} %bitcast.3, bf16[1,3,3,64,64]{4,3,2,1,0:T(8,128)(2,1)} %wa.1, f32[1,2,64]{2,1,0:T(2,128)} %na.1, bf16[3,3,64,128]{3,2,1,0:T(8,128)(2,1)} %wd.1, f32[2,128]{1,0:T(2,128)} %nd.1, bf16[3,3,3,128,128]{4,3,2,1,0:T(8,128)(2,1)} %wb.1, f32[3,2,128]{2,1,0:T(2,128)} %nb.1), custom_call_target="tpu_custom_call" | custom-call | tf_op jit(solution)/shard_map/pallas_call | solution.py:319
  66.5 2.9 %copy.9 = bf16[3,64,32,128]{3,2,1,0:T(8,128)(2,1)} copy(bf16[3,64,32,128]{3,2,1,0:T(8,128)(2,1)} %shard_map.73) | data formatting | bytes 3145728

commit v2 on v0

v2 whole, which is shorter than its diff:
```python
import functools

import jax
import jax.numpy as jnp
from jax import lax
from jax.experimental import pallas as pl
from jax.experimental.pallas import tpu as pltpu
from jax.sharding import PartitionSpec as P

EPS_VALUE = 1e-5
F32 = jnp.float32
BF16 = jnp.bfloat16
NB = 3
MESH = pl.DeviceIdType.MESH


def fused_kernel(dp_size, sp_size, img, wa, na, wd, nd, wb, nb, out,
                 xv, t32, pa0, pa1, za, sa0, sa1, zb, yb0, yb1, wam, wdm, wbm,
                 wav, nav, wdv, ndv, wbv, nbv, st, o32, hs, hr,
                 img_sem, w_sem, st_send, st_recv, halo_send, halo_recv):
    group = dp_size * sp_size
    pod = lax.axis_index("pod")
    dp = lax.axis_index("dp")
    sp = lax.axis_index("sp")
    me = dp * sp_size + sp
    is_top = sp == 0
    is_bottom = sp == sp_size - 1

    dp_order = [dp_size - 1 - dp, lax.rem(dp + 2, dp_size), dp + 1 - 2 * lax.rem(dp, 2), dp]
    sp_order = [lax.rem(sp + off, sp_size) for off in (2, 1, 3, 0)]
    peers = [(pod, d, s) for d in dp_order for s in sp_order][:group - 1]

    barrier = pltpu.get_barrier_semaphore()
    for peer in peers:
        pl.semaphore_signal(barrier, inc=1, device_id=peer, device_id_type=MESH)

    img_copies = [pltpu.make_async_copy(img.at[n], xv.at[n, pl.ds(64, 4096)], img_sem.at[n]) for n in range(NB)]
    w_copies = [pltpu.make_async_copy(src, dst, w_sem.at[i]) for i, (src, dst) in enumerate(
        [(wa, wav), (na, nav), (wd, wdv), (nd, ndv), (wb, wbv), (nb, nbv)])]
    for copy in (w_copies[0], *img_copies, *w_copies[1:]):
        copy.start()

    zero_tile = jnp.zeros((64, 128), BF16)
    zero_row = jnp.zeros((NB, 33, 1, 128), F32)
    for n in range(NB):
        xv[n, 0:64] = zero_tile
        xv[n, 4160:4224] = zero_tile
    t32[:, :, 7:8, :] = zero_row
    t32[:, :, 136:137, :] = zero_row

    w_copies[0].wait()
    zero64 = jnp.zeros((64, 64), BF16)
    for t in range(4):
        for u in range(4):
            parts = []
            for cp in range(2):
                for rp in range(2):
                    p, q = t - rp, u - cp
                    parts.append(wav[0, p, q] if 0 <= p <= 2 and 0 <= q <= 2 else zero64)
            row = t * 256 + u * 64
            wam[row:row + 64, :] = jnp.concatenate(parts, axis=1)

    for n in range(NB):
        img_copies[n].wait()

        def to_rows(i, carry, n=n):
            for j in range(11):
                a = i * 11 + j
                tile = xv[n, pl.ds(pl.multiple_of(a * 128, 128), 128), :]
                t32[n, a, 8:136, :] = tile.T.astype(F32)
            return carry
        lax.fori_loop(0, 3, to_rows, 0)

    def exchange(idx, has_down):
        up = pltpu.make_async_remote_copy(hs.at[idx, 0], hr.at[idx, 1], halo_send.at[idx, 0], halo_recv.at[idx, 0],
                                          device_id=(pod, dp, lax.rem(sp + sp_size - 1, sp_size)), device_id_type=MESH)
        down = None
        if has_down:
            down = pltpu.make_async_remote_copy(hs.at[idx, 1], hr.at[idx, 0], halo_send.at[idx, 1], halo_recv.at[idx, 1],
                                                device_id=(pod, dp, lax.rem(sp + 1, sp_size)), device_id_type=MESH)

        def start():
            @pl.when(sp > 0)
            def _():
                up.start()
            if has_down:
                @pl.when(sp < sp_size - 1)
                def _():
                    down.start()

        def wait():
            @pl.when(sp > 0)
            def _():
                up.wait_send()
                if has_down:
                    down.wait_recv()

            @pl.when(sp < sp_size - 1)
            def _():
                up.wait_recv()
                if has_down:
                    down.wait_send()
        return start, wait

    t_rows = t32.reshape(NB, 33 * 144, 128)
    for n in range(NB):
        hs[0, 0, n, 0:33, :] = t_rows[n, pl.ds(8, 33, stride=144), :]
        hs[0, 1, n, 0:33, :] = t_rows[n, pl.ds(135, 33, stride=144), :]
    pl.semaphore_wait(barrier, group - 1)
    start, wait_image = exchange(0, True)
    start()

    def split_rows(n, a0, dst):
        for j in range(9):
            for t in range(4):
                dst[t, j] = t32[n, a0 + j, pl.ds(7 + t, 64, stride=2), :].astype(BF16)

    def sums(z_val, carry):
        s1, s2 = carry
        z8 = z_val.reshape(-1, 8, 256)
        return s1 + jnp.sum(z8, axis=0), s2 + jnp.sum(z8 * z8, axis=0)

    zero_sums = (jnp.zeros((8, 256), F32), jnp.zeros((8, 256), F32))

    def send_sums(layer, carry):
        rows = []
        for s in carry:
            r = jnp.sum(s, axis=0, keepdims=True)
            rows.append(r[:, :128] + r[:, 128:])
        st[layer, me] = jnp.concatenate(rows, axis=0)
        for peer in peers:
            pltpu.make_async_remote_copy(st.at[layer, me], st.at[layer, me], st_send.at[layer], st_recv.at[layer],
                                         device_id=peer, device_id_type=MESH).start()

    def recv_sums(layer, gamma, beta, count, fold):
        others = st.at[layer, pl.ds(0, group - 1)]
        pltpu.make_async_copy(others, others, st_recv.at[layer]).wait()
        pltpu.make_async_copy(others, others, st_send.at[layer]).wait()
        total = jnp.sum(st[layer], axis=0)
        if fold:
            total = total + pltpu.roll(total, 64, 1)
        mean = total[0:1] / count
        var = total[1:2] / count - mean * mean
        scale = gamma * lax.rsqrt(var + EPS_VALUE)
        return scale, beta - mean * scale

    def conv_a(n, a0, src, carry):
        parts = []
        for t in range(4):
            parts.append(src[t, 0:8].reshape(512, 128))
            parts.append(src[t, 1:9].reshape(512, 128))
        z_val = jnp.dot(jnp.concatenate(parts, axis=1), wam[...], preferred_element_type=F32)
        for cp in range(2):
            za[cp, n, pl.ds(a0, 8), 0:64, :] = z_val[:, cp * 128:cp * 128 + 128].reshape(8, 64, 128)
        return sums(z_val, carry)

    split_rows(0, 0, pa0)

    def loop_a(i, carry):
        n, a0 = lax.div(i, 2), lax.rem(i, 2) * 16
        after = lax.rem(i + 1, 2 * NB)
        carry = conv_a(n, a0, pa0, carry)
        split_rows(n, a0 + 8, pa1)
        carry = conv_a(n, a0 + 8, pa1, carry)
        split_rows(lax.div(after, 2), lax.rem(after, 2) * 16, pa0)
        return carry

    carry = lax.fori_loop(0, 2 * NB, loop_a, zero_sums)

    wait_image()

    @pl.when(is_top)
    def _():
        hr[0, 0] = jnp.zeros(hr.shape[2:], F32)

    @pl.when(is_bottom)
    def _():
        hr[0, 1] = jnp.zeros(hr.shape[2:], F32)

    s1, s2 = carry
    z_rows = za.reshape(2, NB, 32 * 72, 128)
    for n in range(NB):
        for side, row, w_row in ((0, 0, 0), (1, 63, 768)):
            lhs = jnp.concatenate([hr[0, side, n, 0:32, :], hr[0, side, n, 1:33, :]], axis=1).astype(BF16)
            add = jnp.dot(lhs, wam[w_row:w_row + 256, :], preferred_element_type=F32)
            old = jnp.concatenate([z_rows[cp, n, pl.ds(row, 32, stride=72), :] for cp in range(2)], axis=1)
            new = old + add
            for cp in range(2):
                z_rows[cp, n, pl.ds(row, 32, stride=72), :] = new[:, cp * 128:cp * 128 + 128]
            s1 = s1 + jnp.sum(add.reshape(4, 8, 256), axis=0)
            s2 = s2 + jnp.sum((new * new - old * old).reshape(4, 8, 256), axis=0)
    send_sums(0, (s1, s2))
    for n in range(NB):
        for cp in range(2):
            hs[1, 0, n, cp * 32:cp * 32 + 32, :] = z_rows[cp, n, pl.ds(0, 32, stride=72), :]
    start, wait = exchange(1, False)
    start()

    for copy in w_copies[1:]:
        copy.wait()

    def down_tap(v, p):
        cols = []
        for jp in range(2):
            q = v - 2 * jp
            cols.append(wdv[p, q] if 0 <= q <= 2 else jnp.zeros((64, 128), BF16))
        return jnp.concatenate(cols, axis=1)

    for v in range(5):
        for rp in range(2):
            wdm[v * 128 + rp * 64:v * 128 + rp * 64 + 64, :] = down_tap(v, rp)
    for v in range(6):
        wdm[640 + v * 64:640 + v * 64 + 64, :] = down_tap(v, 2)

    def build_b(layer):
        for p in range(3):
            for u in range(4):
                for jp in range(2):
                    q = u - jp
                    blk = wbv[layer, p, q] if 0 <= q <= 2 else jnp.zeros((128, 128), BF16)
                    row = (p * 4 + u) * 128
                    wbm[layer, row:row + 128, jp * 128:jp * 128 + 128] = blk

    for k in (0, 2):
        sa1[k, 8, 0] = zero_tile
    for p in range(3):
        yb0[p, 0, 0] = zero_tile
        yb1[p, 8, 1] = zero_tile

    @pl.when(is_top)
    def _():
        zb[:, :, :, :, 7:8, :] = jnp.zeros((2, 2, NB, 16, 1, 128), F32)

    @pl.when(is_bottom)
    def _():
        hr[1, 1] = jnp.zeros(hr.shape[2:], F32)
        zb[:, :, :, :, 72:73, :] = jnp.zeros((2, 2, NB, 16, 1, 128), F32)

    gamma = jnp.concatenate([nav[0, 0:1, :]] * 2, axis=1)
    beta = jnp.concatenate([nav[0, 1:2, :]] * 2, axis=1)
    wait()
    for n in range(NB):
        for cp in range(2):
            z_rows[cp, n, pl.ds(64, 32, stride=72), :] = hr[1, 1, n, cp * 32:cp * 32 + 32, :]
    scale, shift = recv_sums(0, gamma, beta, float(NB * 128 * 64 * group), True)

    row_idx = lax.broadcasted_iota(jnp.int32, (64, 128), 0)
    lane_idx = lax.broadcasted_iota(jnp.int32, (64, 128), 1)
    low_lanes = lane_idx < 64
    cut_top = jnp.logical_and(row_idx == 0, is_top)
    cut_bottom = jnp.logical_and(row_idx == 63, is_bottom)

    def norm_a(n, half, dst):
        for j in range(17 - half):
            a = half * 16 + j
            for cp in range(2 if j < 16 else 1):
                y = jnp.maximum(za[cp, n, a, 0:64, :] * scale + shift, 0.0)
                dst[cp, j // 2, j % 2] = y.astype(BF16)
            z_next = jnp.where(low_lanes, za[0, n, a, 1:65, :], pltpu.roll(za[1, n, a, 1:65, :], 64, 1))
            y = jnp.maximum(z_next * scale + shift, 0.0)
            dst[2, j // 2, j % 2] = jnp.where(cut_bottom, 0.0, y).astype(BF16)

    def store_z(par, n, g0, z_val):
        for jp in range(2):
            zb[par, jp, n, g0:g0 + 8, 8:72, :] = z_val[:, jp * 128:jp * 128 + 128].reshape(8, 64, 128)

    def conv_down(n, half, src, carry):
        parts = [src[0, 0:8, 0], src[1, 0:8, 0], src[0, 0:8, 1], src[1, 0:8, 1], src[0, 1:9, 0],
                 src[2, 0:8, 0], src[2, 0:8, 1], src[2, 1:9, 0]]
        lhs = jnp.concatenate([x.reshape(512, 128) for x in parts], axis=1)
        z_val = jnp.dot(lhs, wdm[...], preferred_element_type=F32)
        store_z(0, n, half * 8, z_val)
        return sums(z_val, carry)

    norm_a(0, 0, sa0)

    def loop_down(n, carry):
        carry = conv_down(n, 0, sa0, carry)
        norm_a(n, 1, sa1)
        carry = conv_down(n, 1, sa1, carry)
        norm_a(lax.rem(n + 1, NB), 0, sa0)
        return carry

    pixels = float(NB * 64 * 32 * group)
    b_rows = zb.reshape(2, 2, NB, 16 * 80, 128)

    def finish(layer, par, carry, gamma, beta, halo):
        send_sums(layer, carry)
        if halo:
            for n in range(NB):
                for jp in range(2):
                    for side, row in ((0, 8), (1, 71)):
                        hs[layer + 1, side, n, jp * 16:jp * 16 + 16, :] = b_rows[par, jp, n, pl.ds(row, 16, stride=80), :]
            start, wait = exchange(layer + 1, True)
            start()
            build_b(layer - 1)
            wait()

            @pl.when(sp > 0)
            def _():
                for n in range(NB):
                    for jp in range(2):
                        b_rows[par, jp, n, pl.ds(7, 16, stride=80), :] = hr[layer + 1, 0, n, jp * 16:jp * 16 + 16, :]

            @pl.when(sp < sp_size - 1)
            def _():
                for n in range(NB):
                    for jp in range(2):
                        b_rows[par, jp, n, pl.ds(72, 16, stride=80), :] = hr[layer + 1, 1, n, jp * 16:jp * 16 + 16, :]
        return recv_sums(layer, gamma, beta, pixels, False)

    carry = lax.fori_loop(0, NB, loop_down, zero_sums)
    scale, shift = finish(1, 0, carry, ndv[0:1], ndv[1:2], True)

    for layer in range(3):
        par = layer % 2

        def norm_b(n, half, dst, par=par, scale=scale, shift=shift):
            for j in range(1 - half, 18 - half):
                col = half * 16 - 1 + j
                for p in range(3):
                    y = jnp.maximum(zb[par, col % 2, n, col // 2, 7 + p:71 + p, :] * scale + shift, 0.0)
                    if p == 0:
                        y = jnp.where(cut_top, 0.0, y)
                    if p == 2:
                        y = jnp.where(cut_bottom, 0.0, y)
                    dst[p, j // 2, j % 2] = y.astype(BF16)

        def conv_b(n, half, src, carry, layer=layer, par=par):
            parts = []
            for p in range(3):
                for u in range(4):
                    parts.append(src[p, u // 2:u // 2 + 8, u % 2].reshape(512, 128))
            z_val = jnp.dot(jnp.concatenate(parts, axis=1), wbm[layer], preferred_element_type=F32)
            store_z(1 - par, n, half * 8, z_val)
            return sums(z_val, carry)

        norm_b(0, 0, yb0)

        def loop_b(n, carry):
            carry = conv_b(n, 0, yb0, carry)
            norm_b(n, 1, yb1)
            carry = conv_b(n, 1, yb1, carry)
            norm_b(lax.rem(n + 1, NB), 0, yb0)
            return carry

        carry = lax.fori_loop(0, NB, loop_b, zero_sums)
        scale, shift = finish(layer + 2, 1 - par, carry, nbv[layer, 0:1], nbv[layer, 1:2], layer < 2)

    for n in range(NB):
        def norm_out(i, carry, n=n):
            for k in range(4):
                for jp in range(2):
                    g = i * 4 + k
                    y = jnp.maximum(zb[1, jp, n, g, 8:72, :] * scale + shift, 0.0)
                    o32[n, pl.ds(g * 2 + jp, 64, stride=33), :] = y
            return carry
        lax.fori_loop(0, 4, norm_out, 0)

        def pack_out(i, carry, n=n):
            for k in range(8):
                out[n, i * 8 + k] = o32[n, pl.ds((i * 8 + k) * 33, 32), :].astype(BF16)
            return carry
        lax.fori_loop(0, 8, pack_out, 0)


def solution(mesh):
    dp_size, sp_size = mesh.shape["dp"], mesh.shape["sp"]
    group = dp_size * sp_size

    def body(images, w_a, norm_a, w_down, norm_down, w_b, norm_b):
        img = jnp.transpose(images, (0, 2, 3, 1)).reshape(NB, 4096, 128)
        vm = pltpu.VMEM
        hbm_spec = pl.BlockSpec(memory_space=pltpu.HBM)
        return pl.pallas_call(
            functools.partial(fused_kernel, dp_size, sp_size),
            out_shape=jax.ShapeDtypeStruct((NB, 64, 32, 128), BF16),
            in_specs=[hbm_spec] * 7,
            out_specs=pl.BlockSpec(memory_space=pltpu.VMEM),
            scratch_shapes=[
                vm((NB, 4224, 128), BF16),
                vm((NB, 33, 144, 128), F32),
                vm((4, 9, 64, 128), BF16),
                vm((4, 9, 64, 128), BF16),
                vm((2, NB, 32, 72, 128), F32),
                vm((3, 9, 2, 64, 128), BF16),
                vm((3, 9, 2, 64, 128), BF16),
                vm((2, 2, NB, 16, 80, 128), F32),
                vm((3, 9, 2, 64, 128), BF16),
                vm((3, 9, 2, 64, 128), BF16),
                vm((1024, 256), BF16),
                vm((1024, 256), BF16),
                vm((3, 1536, 256), BF16),
                vm((1, 3, 3, 64, 64), BF16),
                vm((1, 2, 64), F32),
                vm((3, 3, 64, 128), BF16),
                vm((2, 128), F32),
                vm((3, 3, 3, 128, 128), BF16),
                vm((3, 2, 128), F32),
                vm((5, group, 2, 128), F32),
                vm((NB, 64 * 33, 128), F32),
                vm((5, 2, NB, 64, 128), F32),
                vm((5, 2, NB, 64, 128), F32),
                pltpu.SemaphoreType.DMA((NB,)),
                pltpu.SemaphoreType.DMA((6,)),
                pltpu.SemaphoreType.DMA((5,)),
                pltpu.SemaphoreType.DMA((5,)),
                pltpu.SemaphoreType.DMA((5, 2)),
                pltpu.SemaphoreType.DMA((5, 2)),
            ],
            compiler_params=pltpu.CompilerParams(
                collective_id=0, has_side_effects=True, vmem_limit_bytes=48 * 1024 * 1024),
        )(*[pltpu.with_memory_space_constraint(x, pltpu.HBM) for x in (img, w_a, norm_a, w_down, norm_down, w_b, norm_b)])

    act_spec = P(("pod", "dp"), "sp", None, None)
    return jax.shard_map(body, mesh=mesh, in_specs=(act_spec, P(), P(), P(), P(), P(), P()), out_specs=act_spec, check_vma=False)
```

time: 369 us -> 47.7 us (0.13); the launches traced: 364 us -> 47.6 us
  blocking collectives: 156 us -> 0 us
  local copies, waits for them, and re-layouts: 89 us -> 1.15 us
  other arithmetic: 49.9 us -> 0 us
  matrix products: 47.7 us -> 0 us
  Pallas kernels: 0 us -> 46.4 us
  starting transfers between devices: 19.3 us -> 0 us
    psum x5 -> x0, blocking collectives: 156 us -> none  [batch_norm(): group_sums = lax.psum(local_sums, ('dp', 'sp'))]
    conv_general_dilated x5 -> x0, matrix products: 47.7 us -> none  [the longest x4 39.6 us: same_layer(): lax.conv_general_dilated(padded, weight, (1, 1), ((0, 0), (1, 1)), dimens...]
    pallas_call x0 -> x1, Pallas kernels: none -> 46.4 us  [body(): pl.pallas_call(functools.partial(fused_kernel, dp_size, sp_size), out_sha...]
    conv_general_dilated x8 -> x0, local copies, waits for them, and re-layouts: 46.3 us -> none  [the longest x6 29.1 us: same_layer(): lax.conv_general_dilated(padded, weight, (1, 1), ((0, 0), (1, 1)), dimens...]
    convert_element_type x5 -> x0, other arithmetic: 21.7 us -> none  [batch_norm(): return jnp.maximum(scaled, 0.0).astype(jnp.bfloat16)]
    ppermute x9 -> x0, starting transfers between devices: 19.3 us -> none  [the longest x4 12.3 us: same_layer(): top_rows = lax.ppermute(hidden[:, -1:], 'sp', to_lower)]
    concatenate x5 -> x0, other arithmetic: 16.1 us -> none  [the longest x4 9.13 us: same_layer(): padded = jnp.concatenate([top_rows, hidden, bottom_rows], axis=1)]
    concatenate x5 -> x0, local copies, waits for them, and re-layouts: 10.3 us -> none  [the longest x4 5.68 us: same_layer(): padded = jnp.concatenate([top_rows, hidden, bottom_rows], axis=1)]
  transfers between devices with their start and end apart: 9 -> 0, of which waited for: 4 -> 0; matrix products, arithmetic and copies ran while one was open for 2% -> 0% of each run, Pallas kernels for 0% -> 0%
where the time goes in v2:
time: 47.7 us; the launch traced here: 47.6 us
  Pallas kernels  46.4 us (97%)
  local copies, waits for them, and re-layouts  1.15 us (2%)
    pallas_call x1, Pallas kernels, body(): pl.pallas_call(functools.partial(fused_kernel, dp_size, sp_size), out_sha...  46.4 us
    unnamed x1, local copies, waits for them, and re-layouts  1.15 us

profile of v2, /device:TPU:0, one launch (start us, length us, event | category | flops | bytes accessed | tf_op | source)
XLA Modules:
  0.0 47.6 jit_solution(3484893278396101300)
XLA Ops:
  0.0 46.4 %shard_map.73 = bf16[3,64,32,128]{3,2,1,0:T(8,128)(2,1)S(1)} custom-call(bf16[3,4096,128]{2,1,0:T(8,128)(2,1)} %bitcast.3, bf16[1,3,3,64,64]{4,3,2,1,0:T(8,128)(2,1)} %wa.1, f32[1,2,64]{2,1,0:T(2,128)} %na.1, bf16[3,3,64,128]{3,2,1,0:T(8,128)(2,1)} %wd.1, f32[2,128]{1,0:T(2,128)} %nd.1, bf16[3,3,3,128,128]{4,3,2,1,0:T(8,128)(2,1)} %wb.1, f32[3,2,128]{2,1,0:T(2,128)} %nb.1), custom_call_target="tpu_custom_call" | custom-call | tf_op jit(solution)/shard_map/pallas_call | solution.py:375
  46.4 1.1 %copy.9 = bf16[3,64,32,128]{3,2,1,0:T(8,128)(2,1)} copy(bf16[3,64,32,128]{3,2,1,0:T(8,128)(2,1)S(1)} %shard_map.73) | data formatting | bytes 3145728

commit v3 on v2

--- a/solution.py
+++ b/solution.py
@@ -165,7 +165,7 @@
         split_rows(lax.div(after, 2), lax.rem(after, 2) * 16, pa0)
         return carry
 
-    carry = lax.fori_loop(0, 2 * NB, loop_a, zero_sums)
+    carry = lax.fori_loop(0, 2 * NB, loop_a, zero_sums, unroll=True)
 
     wait_image()
 
@@ -309,7 +309,7 @@
                         b_rows[par, jp, n, pl.ds(72, 16, stride=80), :] = hr[layer + 1, 1, n, jp * 16:jp * 16 + 16, :]
         return recv_sums(layer, gamma, beta, pixels, False)
 
-    carry = lax.fori_loop(0, NB, loop_down, zero_sums)
+    carry = lax.fori_loop(0, NB, loop_down, zero_sums, unroll=True)
     scale, shift = finish(1, 0, carry, ndv[0:1], ndv[1:2], True)
 
     for layer in range(3):
@@ -344,7 +344,7 @@
             norm_b(lax.rem(n + 1, NB), 0, yb0)
             return carry
 
-        carry = lax.fori_loop(0, NB, loop_b, zero_sums)
+        carry = lax.fori_loop(0, NB, loop_b, zero_sums, unroll=True)
         scale, shift = finish(layer + 2, 1 - par, carry, nbv[layer, 0:1], nbv[layer, 1:2], layer < 2)
 
     for n in range(NB):

time: 47.7 us -> 43.3 us (0.908)
  Pallas kernels: 46.4 us -> 42 us
    pallas_call x1, Pallas kernels: 46.4 us -> 42 us  [body(): pl.pallas_call(functools.partial(fused_kernel, dp_size, sp_size), out_sha...]
where the time goes in v3:
time: 43.3 us; the launch traced here: 43.1 us
  Pallas kernels  42 us (97%)
  local copies, waits for them, and re-layouts  1.15 us (3%)
    pallas_call x1, Pallas kernels, body(): pl.pallas_call(functools.partial(fused_kernel, dp_size, sp_size), out_sha...  42 us
    unnamed x1, local copies, waits for them, and re-layouts  1.15 us

profile of v3, /device:TPU:0, one launch (start us, length us, event | category | flops | bytes accessed | tf_op | source)
XLA Modules:
  0.0 43.1 jit_solution(4084497007288792748)
XLA Ops:
  0.0 42.0 %shard_map.73 = bf16[3,64,32,128]{3,2,1,0:T(8,128)(2,1)S(1)} custom-call(bf16[3,4096,128]{2,1,0:T(8,128)(2,1)} %bitcast.3, bf16[1,3,3,64,64]{4,3,2,1,0:T(8,128)(2,1)} %wa.1, f32[1,2,64]{2,1,0:T(2,128)} %na.1, bf16[3,3,64,128]{3,2,1,0:T(8,128)(2,1)} %wd.1, f32[2,128]{1,0:T(2,128)} %nd.1, bf16[3,3,3,128,128]{4,3,2,1,0:T(8,128)(2,1)} %wb.1, f32[3,2,128]{2,1,0:T(2,128)} %nb.1), custom_call_target="tpu_custom_call" | custom-call | tf_op jit(solution)/shard_map/pallas_call | solution.py:375
  42.0 1.1 %copy.9 = bf16[3,64,32,128]{3,2,1,0:T(8,128)(2,1)} copy(bf16[3,64,32,128]{3,2,1,0:T(8,128)(2,1)S(1)} %shard_map.73) | data formatting | bytes 3145728

commit v4 on v3

--- a/solution.py
+++ b/solution.py
@@ -60,16 +60,12 @@
             row = t * 256 + u * 64
             wam[row:row + 64, :] = jnp.concatenate(parts, axis=1)
 
-    for n in range(NB):
-        img_copies[n].wait()
-
-        def to_rows(i, carry, n=n):
-            for j in range(11):
-                a = i * 11 + j
-                tile = xv[n, pl.ds(pl.multiple_of(a * 128, 128), 128), :]
-                t32[n, a, 8:136, :] = tile.T.astype(F32)
-            return carry
-        lax.fori_loop(0, 3, to_rows, 0)
+    def to_rows(n, first, last):
+        for a in range(first, last):
+            t32[n, a, 8:136, :] = xv[n, a * 128:a * 128 + 128, :].T.astype(F32)
+
+    img_copies[0].wait()
+    to_rows(0, 0, 33)
 
     def exchange(idx, has_down):
         up = pltpu.make_async_remote_copy(hs.at[idx, 0], hr.at[idx, 1], halo_send.at[idx, 0], halo_recv.at[idx, 0],
@@ -101,14 +97,6 @@
                 if has_down:
                     down.wait_send()
         return start, wait
-
-    t_rows = t32.reshape(NB, 33 * 144, 128)
-    for n in range(NB):
-        hs[0, 0, n, 0:33, :] = t_rows[n, pl.ds(8, 33, stride=144), :]
-        hs[0, 1, n, 0:33, :] = t_rows[n, pl.ds(135, 33, stride=144), :]
-    pl.semaphore_wait(barrier, group - 1)
-    start, wait_image = exchange(0, True)
-    start()
 
     def split_rows(n, a0, dst):
         for j in range(9):
@@ -151,21 +139,29 @@
             parts.append(src[t, 1:9].reshape(512, 128))
         z_val = jnp.dot(jnp.concatenate(parts, axis=1), wam[...], preferred_element_type=F32)
         for cp in range(2):
-            za[cp, n, pl.ds(a0, 8), 0:64, :] = z_val[:, cp * 128:cp * 128 + 128].reshape(8, 64, 128)
+            za[cp, n, a0:a0 + 8, 0:64, :] = z_val[:, cp * 128:cp * 128 + 128].reshape(8, 64, 128)
         return sums(z_val, carry)
 
     split_rows(0, 0, pa0)
-
-    def loop_a(i, carry):
-        n, a0 = lax.div(i, 2), lax.rem(i, 2) * 16
-        after = lax.rem(i + 1, 2 * NB)
-        carry = conv_a(n, a0, pa0, carry)
-        split_rows(n, a0 + 8, pa1)
-        carry = conv_a(n, a0 + 8, pa1, carry)
-        split_rows(lax.div(after, 2), lax.rem(after, 2) * 16, pa0)
-        return carry
-
-    carry = lax.fori_loop(0, 2 * NB, loop_a, zero_sums, unroll=True)
+    img_copies[1].wait()
+    t_rows = t32.reshape(NB, 33 * 144, 128)
+    carry = zero_sums
+    blocks = [(n, a0) for n in range(NB) for a0 in range(0, 32, 8)]
+    for i, (n, a0) in enumerate(blocks):
+        if i == 2:
+            img_copies[2].wait()
+        if i == 4:
+            for k in range(NB):
+                hs[0, 0, k, 0:33, :] = t_rows[k, pl.ds(8, 33, stride=144), :]
+                hs[0, 1, k, 0:33, :] = t_rows[k, pl.ds(135, 33, stride=144), :]
+            pl.semaphore_wait(barrier, group - 1)
+            start, wait_image = exchange(0, True)
+            start()
+        carry = conv_a(n, a0, (pa0, pa1)[i % 2], carry)
+        if i < 4:
+            to_rows(1 + i // 2, (0, 17)[i % 2], (17, 33)[i % 2])
+        if i + 1 < len(blocks):
+            split_rows(*blocks[i + 1], (pa1, pa0)[i % 2])
 
     wait_image()
 

time: 43.3 us -> 42.7 us (0.986)
  Pallas kernels: 42 us -> 41.4 us
    pallas_call x1, Pallas kernels: 42 us -> 41.4 us  [body(): pl.pallas_call(functools.partial(fused_kernel, dp_size, sp_size), out_sha...]
where the time goes in v4:
time: 42.7 us; the launch traced here: 42.5 us
  Pallas kernels  41.4 us (97%)
  local copies, waits for them, and re-layouts  1.15 us (3%)
    pallas_call x1, Pallas kernels, body(): pl.pallas_call(functools.partial(fused_kernel, dp_size, sp_size), out_sha...  41.4 us
    unnamed x1, local copies, waits for them, and re-layouts  1.15 us

profile of v4, /device:TPU:0, one launch (start us, length us, event | category | flops | bytes accessed | tf_op | source)
XLA Modules:
  0.0 42.5 jit_solution(14285135791607665713)
XLA Ops:
  0.0 41.4 %shard_map.73 = bf16[3,64,32,128]{3,2,1,0:T(8,128)(2,1)S(1)} custom-call(bf16[3,4096,128]{2,1,0:T(8,128)(2,1)} %bitcast.3, bf16[1,3,3,64,64]{4,3,2,1,0:T(8,128)(2,1)} %wa.1, f32[1,2,64]{2,1,0:T(2,128)} %na.1, bf16[3,3,64,128]{3,2,1,0:T(8,128)(2,1)} %wd.1, f32[2,128]{1,0:T(2,128)} %nd.1, bf16[3,3,3,128,128]{4,3,2,1,0:T(8,128)(2,1)} %wb.1, f32[3,2,128]{2,1,0:T(2,128)} %nb.1), custom_call_target="tpu_custom_call" | custom-call | tf_op jit(solution)/shard_map/pallas_call | solution.py:371
  41.4 1.1 %copy.9 = bf16[3,64,32,128]{3,2,1,0:T(8,128)(2,1)} copy(bf16[3,64,32,128]{3,2,1,0:T(8,128)(2,1)S(1)} %shard_map.73) | data formatting | bytes 3145728

commit v5 on v4

--- a/solution.py
+++ b/solution.py
@@ -274,7 +274,8 @@
         carry = conv_down(n, 0, sa0, carry)
         norm_a(n, 1, sa1)
         carry = conv_down(n, 1, sa1, carry)
-        norm_a(lax.rem(n + 1, NB), 0, sa0)
+        if n + 1 < NB:
+            norm_a(n + 1, 0, sa0)
         return carry
 
     pixels = float(NB * 64 * 32 * group)
@@ -305,7 +306,9 @@
                         b_rows[par, jp, n, pl.ds(72, 16, stride=80), :] = hr[layer + 1, 1, n, jp * 16:jp * 16 + 16, :]
         return recv_sums(layer, gamma, beta, pixels, False)
 
-    carry = lax.fori_loop(0, NB, loop_down, zero_sums, unroll=True)
+    carry = zero_sums
+    for n in range(NB):
+        carry = loop_down(n, carry)
     scale, shift = finish(1, 0, carry, ndv[0:1], ndv[1:2], True)
 
     for layer in range(3):
@@ -337,10 +340,13 @@
             carry = conv_b(n, 0, yb0, carry)
             norm_b(n, 1, yb1)
             carry = conv_b(n, 1, yb1, carry)
-            norm_b(lax.rem(n + 1, NB), 0, yb0)
+            if n + 1 < NB:
+                norm_b(n + 1, 0, yb0)
             return carry
 
-        carry = lax.fori_loop(0, NB, loop_b, zero_sums, unroll=True)
+        carry = zero_sums
+        for n in range(NB):
+            carry = loop_b(n, carry)
         scale, shift = finish(layer + 2, 1 - par, carry, nbv[layer, 0:1], nbv[layer, 1:2], layer < 2)
 
     for n in range(NB):

time: 42.7 us -> 42.4 us (level)
  no operation moved by 1% of the time
where the time goes in v5:
time: 42.4 us; the launch traced here: 42.3 us
  Pallas kernels  41.1 us (97%)
  local copies, waits for them, and re-layouts  1.15 us (3%)
    pallas_call x1, Pallas kernels, body(): pl.pallas_call(functools.partial(fused_kernel, dp_size, sp_size), out_sha...  41.1 us
    unnamed x1, local copies, waits for them, and re-layouts  1.15 us

profile of v5, /device:TPU:0, one launch (start us, length us, event | category | flops | bytes accessed | tf_op | source)
XLA Modules:
  0.0 42.3 jit_solution(6120567387249652781)
XLA Ops:
  0.0 41.1 %shard_map.73 = bf16[3,64,32,128]{3,2,1,0:T(8,128)(2,1)S(1)} custom-call(bf16[3,4096,128]{2,1,0:T(8,128)(2,1)} %bitcast.3, bf16[1,3,3,64,64]{4,3,2,1,0:T(8,128)(2,1)} %wa.1, f32[1,2,64]{2,1,0:T(2,128)} %na.1, bf16[3,3,64,128]{3,2,1,0:T(8,128)(2,1)} %wd.1, f32[2,128]{1,0:T(2,128)} %nd.1, bf16[3,3,3,128,128]{4,3,2,1,0:T(8,128)(2,1)} %wb.1, f32[3,2,128]{2,1,0:T(2,128)} %nb.1), custom_call_target="tpu_custom_call" | custom-call | tf_op jit(solution)/shard_map/pallas_call | solution.py:377
  41.1 1.1 %copy.9 = bf16[3,64,32,128]{3,2,1,0:T(8,128)(2,1)} copy(bf16[3,64,32,128]{3,2,1,0:T(8,128)(2,1)S(1)} %shard_map.73) | data formatting | bytes 3145728
